TPU v7x, 32 devices: a whole 2x2x4 slice. The times are simulated.
32 devices in a mesh: dp: 8 (over y, x, core), seq: 4 (over z).
Axes of the slice: x: 2, y: 2, z: 4, core: 2. Of those that a mesh axis runs over, the one named last changes fastest.
Arguments:
- tokens: bfloat16 [8, 512, 2048], P('dp', 'seq'), may hold values from -6 to 6
- qkv_weight: bfloat16 [3, 2048, 1024], P(None, 'dp', 'seq'), may hold values from -0.125 to 0.125
- qk_scale: float32 [1024], replicated, may hold values from 0.5 to 10
- out_weight: bfloat16 [1024, 2048], P('seq', 'dp'), may hold values from -0.1875 to 0.1875
- mix_rates: float32 [2, 2048], replicated, may hold values from 0.1 to 0.6
- gate_up_weight: bfloat16 [2, 2048, 8192], P(None, 'dp', 'seq'), may hold values from -0.125 to 0.125
- mlp_scales: float32 [2, 8192], P(None, 'seq'), may hold values from 0.5 to 2
- down_weight: bfloat16 [8192, 2048], P('seq', 'dp'), may hold values from -0.0625 to 0.0625
Outputs:
- result: bfloat16 [8, 512, 2048], P('dp', 'seq')
All inputs are finite; a program needn't handle non-finite values.
Results may differ from a plain program's by a relative error of at most 0.015.
The roundings to bfloat16 on the way count: a program that leaves them out, or rounds other values in their place, can miss the bound.
Values may be sent and summed in bfloat16 or wider, within the bound.
No kernel may reach another device: no remote copies, remote signals or barrier semaphores. Data moves between devices by JAX's collectives and lax.ppermute only.
A program may use at most 128 MiB of HBM per device.

v0:
```python
import jax
import jax.numpy as jnp
from jax import lax
from jax.sharding import PartitionSpec as P

HD = 128


def unit_rms(values_in):
    return values_in * lax.rsqrt(jnp.mean(values_in * values_in, axis=-1, keepdims=True) + 1e-06)


def prepare(projected, scale_heads):
    queries = unit_rms(projected[:, 0]) * scale_heads
    key_rows = unit_rms(projected[:, 1]) * scale_heads
    return jnp.stack([queries, key_rows, projected[:, 2]], axis=1).astype(jnp.bfloat16)


def attend(stacked):
    length = stacked.shape[0]
    head_count = stacked.shape[2]
    head_dim = stacked.shape[3]
    block_rows = min(length, 512)
    block_count = length // block_rows
    key_rows = stacked[:, 1]
    value_rows = stacked[:, 2]
    queries = stacked[:, 0].reshape(block_count, block_rows, head_count, head_dim)
    positions = jnp.arange(length, dtype=jnp.int32)
    factor = head_dim ** (-0.5)

    def one_block(inputs):
        block_index, query_block = inputs
        scores = (
            jnp.einsum("qhd,khd->hqk", query_block, key_rows, preferred_element_type=jnp.float32)
            * factor
        )
        query_pos = block_index * block_rows + jnp.arange(block_rows, dtype=jnp.int32)
        allowed = positions[None, :] <= query_pos[:, None]
        scores = jnp.where(allowed[None], scores, -1e30)
        highest = jnp.max(scores, axis=-1, keepdims=True)
        powers = jnp.exp(scores - highest)
        shares = (powers / jnp.sum(powers, axis=-1, keepdims=True)).astype(jnp.bfloat16)
        mixed = jnp.einsum("hqk,khd->qhd", shares, value_rows, preferred_element_type=jnp.float32)
        return mixed.astype(jnp.bfloat16)

    mixed_all = lax.map(one_block, (jnp.arange(block_count, dtype=jnp.int32), queries))
    return mixed_all.reshape(length, head_count, head_dim)


def on_device(
    tokens, qkv_weight, qk_scale, out_weight, mix_rates, gate_up_weight, mlp_scales, down_weight
):
    own_rows = tokens[0]
    head_dim = HD
    normed = unit_rms(own_rows.astype(jnp.float32)).astype(jnp.bfloat16)
    scale_all = qk_scale.reshape(-1, head_dim)
    sequence = lax.all_gather(normed, "seq", axis=0, tiled=True)
    length = sequence.shape[0]
    columns = sequence
    projected = jnp.einsum(
        "td,cdn->tcn",
        columns,
        lax.all_gather(qkv_weight, "dp", axis=1, tiled=True),
        preferred_element_type=jnp.float32,
    )
    local_heads = qkv_weight.shape[2] // head_dim
    scale_local = lax.dynamic_slice_in_dim(
        scale_all, lax.axis_index("seq") * local_heads, local_heads, 0
    )
    stacked = prepare(projected.reshape(length, 3, local_heads, head_dim), scale_local)
    attended = attend(stacked).reshape(length, -1)
    out_cols_all = lax.all_gather(out_weight, "dp", axis=1, tiled=True)
    part_rows = attended
    attention = lax.psum_scatter(
        jnp.dot(part_rows, out_cols_all, preferred_element_type=jnp.float32).astype(jnp.bfloat16),
        "seq",
        scatter_dimension=0,
        tiled=True,
    ).astype(jnp.float32)
    normed_f = normed.astype(jnp.float32)
    middle = unit_rms(normed_f + mix_rates[0] * (unit_rms(attention) - normed_f)).astype(
        jnp.bfloat16
    )
    sequence_mid = lax.all_gather(middle, "seq", axis=0, tiled=True)
    columns = sequence_mid
    gate_up = jnp.einsum(
        "td,cdf->tcf",
        columns,
        lax.all_gather(gate_up_weight, "dp", axis=1, tiled=True),
        preferred_element_type=jnp.float32,
    )
    hidden = (jax.nn.silu(gate_up[:, 0] * mlp_scales[0]) * (gate_up[:, 1] * mlp_scales[1])).astype(
        jnp.bfloat16
    )
    down_all = lax.all_gather(down_weight, "dp", axis=1, tiled=True)
    part_rows = hidden
    feed_out = lax.psum_scatter(
        jnp.dot(part_rows, down_all, preferred_element_type=jnp.float32).astype(jnp.bfloat16),
        "seq",
        scatter_dimension=0,
        tiled=True,
    ).astype(jnp.float32)
    middle_f = middle.astype(jnp.float32)
    result = unit_rms(middle_f + mix_rates[1] * (unit_rms(feed_out) - middle_f)).astype(
        jnp.bfloat16
    )
    return result[None]


def solution(mesh):
    return jax.shard_map(
        on_device,
        mesh=mesh,
        in_specs=(
            P("dp", "seq", None),
            P(None, "dp", "seq"),
            P(),
            P("seq", "dp"),
            P(),
            P(None, "dp", "seq"),
            P(None, "seq"),
            P("seq", "dp"),
        ),
        out_specs=P("dp", "seq", None),
        check_vma=False,
    )
```

profile of v0, /device:TPU:0, one launch (start us, length us, event | category | flops | bytes accessed | tf_op | source)
XLA Modules:
  0.0 430.2 jit_solution(14153458220697589885)
XLA Ops:
  6.5 1.3 fusion.17
  7.8 2.0 fusion.18
  9.8 0.0 all-gather.9.cloned.1.call-start
  9.9 0.9 copy.9
  10.9 0.7 all-gather.11.cloned.1.call-update
  11.7 0.1 iota_compare_fusion
  11.8 46.6 %all-gather.7.cloned.1.call-done = bf16[512,2048]{1,0:T(8,128)(2,1)} async-done(((bf16[128,2048]{1,0:T(8,128)(2,1)}), bf16[512,2048]{1,0:T(8,128)(2,1)}) %all-gather.7.cloned.1.call-update) | async-done | bytes 2097168 | tf_op jit(solution)/shard_map/all_gather | solution.py:57
  58.4 33.4 %all-gather.9.cloned.1.call-done = bf16[3,2048,256]{1,2,0:T(8,128)(2,1)} async-done(((bf16[3,256,256]{1,2,0:T(8,128)(2,1)}), bf16[3,2048,256]{1,2,0:T(8,128)(2,1)}) %all-gather.9.cloned.1.call-update) | async-done | bytes 3145744 | tf_op jit(solution)/shard_map/all_gather | solution.py:63
  91.8 4.3 %fusion.7 = f32[512,3,256]{0,2,1:T(8,128)S(1)} fusion(bf16[3,2048,256]{1,2,0:T(8,128)(2,1)} %all-gather.9.cloned.1.call-done, bf16[512,2048]{1,0:T(8,128)(2,1)} %all-gather.7.cloned.1.call-done), kind=kOutput, calls=%fused_computation.11 | convolution fusion | flops 1610612736 | bytes 6815744 | tf_op jit(solution)/shard_map/td,cdn->tcn/dot_general | solution.py:60
  96.2 0.1 multiply_reduce_fusion.3
  96.3 1.1 fusion.63
  97.4 1.3 convolution_convert_fusion.2
  98.7 18.5 %all-gather.11.cloned.1.call-done = bf16[256,2048]{1,0:T(8,128)(2,1)} async-done(((bf16[256,256]{1,0:T(8,128)(2,1)}), bf16[256,2048]{1,0:T(8,128)(2,1)}) %all-gather.11.cloned.1.call-update) | async-done | bytes 1048592 | tf_op jit(solution)/shard_map/all_gather | solution.py:72
  117.2 3.3 convolution_convert_fusion
  120.6 0.0 all-gather.13.cloned.1.call-start
  120.6 0.6 copy-done.4
  121.3 43.1 %reduce-scatter.3.cloned.1.call-done = bf16[128,2048]{1,0:T(8,128)(2,1)} async-done(((bf16[512,2048]{1,0:T(8,128)(2,1)}), bf16[128,2048]{1,0:T(8,128)(2,1)}) %reduce-scatter.3.cloned.1.call-update) | async-done | bytes 524304 | tf_op jit(solution)/shard_map/reduce_scatter | solution.py:74
  164.4 1.2 fusion.14
  165.6 1.5 multiply_reduce_fusion.1
  167.1 2.2 multiply_convert_fusion.1
  169.4 0.5 all-gather.15.cloned.1.call-update
  170.0 0.7 all-gather.17.cloned.1.call-update
  170.7 0.2 reduce-scatter.5.cloned.1.call-start
  171.0 43.4 %all-gather.13.cloned.1.call-done = bf16[512,2048]{1,0:T(8,128)(2,1)} async-done(((bf16[128,2048]{1,0:T(8,128)(2,1)}), bf16[512,2048]{1,0:T(8,128)(2,1)}) %all-gather.13.cloned.1.call-update) | async-done | bytes 2097168 | tf_op jit(solution)/shard_map/all_gather | solution.py:84
  214.4 90.3 %all-gather.15.cloned.1.call-done = bf16[2,2048,2048]{2,1,0:T(8,128)(2,1)} async-done(((bf16[2,256,2048]{2,1,0:T(8,128)(2,1)}), bf16[2,2048,2048]{2,1,0:T(8,128)(2,1)}) %all-gather.15.cloned.1.call-update) | async-done | bytes 16777232 | tf_op jit(solution)/shard_map/all_gather | solution.py:89
  304.7 14.9 %fusion.5 = f32[512,2,2048]{2,0,1:T(8,128)} fusion(bf16[2,2048,2048]{2,1,0:T(8,128)(2,1)} %all-gather.15.cloned.1.call-done, bf16[512,2048]{1,0:T(8,128)(2,1)} %all-gather.13.cloned.1.call-done), kind=kOutput, calls=%fused_computation.9 | convolution fusion | flops 8589934592 | bytes 27262976 | tf_op jit(solution)/shard_map/td,cdf->tcf/dot_general | solution.py:86
  319.6 42.9 %all-gather.17.cloned.1.call-done = bf16[2048,2048]{1,0:T(8,128)(2,1)} async-done(((bf16[2048,256]{1,0:T(8,128)(2,1)}), bf16[2048,2048]{1,0:T(8,128)(2,1)}) %all-gather.17.cloned.1.call-update) | async-done | bytes 8388624 | tf_op jit(solution)/shard_map/all_gather | solution.py:95
  362.5 11.9 %convolution_convert_fusion.1 = bf16[512,2048]{1,0:T(8,128)(2,1)} fusion(bf16[2048,2048]{1,0:T(8,128)(2,1)} %all-gather.17.cloned.1.call-done, f32[512,2,2048]{2,0,1:T(8,128)} %fusion.5, f32[2048]{0:T(1024)S(1)} %bitcast.89, f32[2048]{0:T(1024)S(1)} %bitcast.88), kind=kOutput, calls=%fused_computation.8 | convolution fusion | flops 4304404480 | bytes 18890752 | tf_op jit(solution)/shard_map/dot_general | solution.py:98
  374.4 43.8 %reduce-scatter.5.cloned.1.call-done = bf16[128,2048]{1,0:T(8,128)(2,1)} async-done(((bf16[512,2048]{1,0:T(8,128)(2,1)}), bf16[128,2048]{1,0:T(8,128)(2,1)}) %reduce-scatter.5.cloned.1.call-update) | async-done | bytes 524304 | tf_op jit(solution)/shard_map/reduce_scatter | solution.py:97
  418.2 1.2 fusion.16
  419.5 1.5 multiply_reduce_fusion
  421.0 2.3 fusion.22
  (30 shorter events, 0.4 us)
Async XLA Ops:
  6.5 5.1 %copy-start = (f32[1024]{0:T(1024)S(1)}, f32[1024]{0:T(1024)}, u32[]{:S(2)}) copy-start(f32[1024]{0:T(1024)} %param.10) | copy-start | bytes 12292
  6.5 3.4 copy-start.3
  6.5 51.8 %all-gather.7.cloned.1.call-start = ((), (), s32[]{:S(2)}) async-start(), calls=%async_computation.2 | async-start | bytes 2621440 | tf_op jit(solution)/shard_map/all_gather | solution.py:57
  9.8 82.0 %all-gather.9.cloned.1.call-start = ((), (), s32[]{:S(2)}) async-start(), calls=%async_computation.3 | async-start | bytes 3538944 | tf_op jit(solution)/shard_map/all_gather | solution.py:63
  10.9 106.3 %all-gather.11.cloned.1.call-start = ((), (), s32[]{:S(2)}) async-start(), calls=%async_computation.4 | async-start | bytes 1179648 | tf_op jit(solution)/shard_map/all_gather | solution.py:72
  11.6 152.7 %reduce-scatter.3.cloned.1.call-start = ((), (), s32[]{:S(2)}) async-start(), calls=%async_computation.5 | async-start | bytes 2621440 | tf_op jit(solution)/shard_map/reduce_scatter | solution.py:74
  120.5 0.7 copy-start.4
  120.5 45.1 %copy-start.1 = (bf16[1,128,2048]{2,1,0:T(8,128)(2,1)S(1)}, bf16[1,128,2048]{2,1,0:T(8,128)(2,1)}, u32[]{:S(2)}) copy-start(bf16[1,128,2048]{2,1,0:T(8,128)(2,1)} %param.8) | copy-start | bytes 1572868
  120.6 93.8 %all-gather.13.cloned.1.call-start = ((), (), s32[]{:S(2)}) async-start(), calls=%async_computation.6 | async-start | bytes 2621440 | tf_op jit(solution)/shard_map/all_gather | solution.py:84
  169.3 1.6 copy-start.5
  169.4 135.3 %all-gather.15.cloned.1.call-start = ((), (), s32[]{:S(2)}) async-start(), calls=%async_computation.7 | async-start | bytes 18874368 | tf_op jit(solution)/shard_map/all_gather | solution.py:89
  169.9 192.5 %all-gather.17.cloned.1.call-start = ((), (), s32[]{:S(2)}) async-start(), calls=%async_computation.8 | async-start | bytes 9437184 | tf_op jit(solution)/shard_map/all_gather | solution.py:95
  170.7 247.5 %reduce-scatter.5.cloned.1.call-start = ((), (), s32[]{:S(2)}) async-start(), calls=%async_computation.9 | async-start | bytes 2621440 | tf_op jit(solution)/shard_map/reduce_scatter | solution.py:97
  374.4 45.1 %copy-start.2 = (bf16[128,2048]{1,0:T(8,128)(2,1)S(1)}, bf16[128,2048]{1,0:T(8,128)(2,1)}, u32[]{:S(2)}) copy-start(bf16[128,2048]{1,0:T(8,128)(2,1)} %multiply_convert_fusion.1) | copy-start | bytes 1572868
Sparse Core Ops, SparseCore 0:
  10.0 48.3 all-gather.6
  60.3 31.5 all-gather.8
  93.7 23.4 all-gather.10
  120.7 43.6 reduce-scatter.2
  169.5 44.8 all-gather.12
  216.1 88.5 all-gather.14
  306.6 55.8 all-gather.16
  374.5 43.6 reduce-scatter.4
where the time goes:
time: 431 us; the launch traced here: 430 us
  waiting for transfers between devices  364 us (84%)
  matrix products  36.9 us (9%)
  between operations  13.6 us (3%)
  other arithmetic  13.5 us (3%)
    all_gather x1, waiting for transfers between devices, on_device(): lax.all_gather(gate_up_weight, 'dp', axis=1, tiled=True)  90.3 us
    all_gather x1, waiting for transfers between devices, on_device(): sequence = lax.all_gather(normed, 'seq', axis=0, tiled=True)  46.6 us
    reduce_scatter x1, waiting for transfers between devices, on_device(): lax.psum_scatter(jnp.dot(part_rows, down_all, preferred_element_type=jnp....  43.8 us
    all_gather x1, waiting for transfers between devices, on_device(): sequence_mid = lax.all_gather(middle, 'seq', axis=0, tiled=True)  43.4 us
    reduce_scatter x1, waiting for transfers between devices, on_device(): lax.psum_scatter(jnp.dot(part_rows, out_cols_all, preferred_element_type=...  43.1 us
    all_gather x1, waiting for transfers between devices, on_device(): down_all = lax.all_gather(down_weight, 'dp', axis=1, tiled=True)  42.9 us
    all_gather x1, waiting for transfers between devices, on_device(): lax.all_gather(qkv_weight, 'dp', axis=1, tiled=True)  33.4 us
    all_gather x1, waiting for transfers between devices, on_device(): out_cols_all = lax.all_gather(out_weight, 'dp', axis=1, tiled=True)  18.5 us
  transfers between devices with their start and end apart: 8, of which 8 were waited for; matrix products, arithmetic and copies ran while one was open for 5% of the time, Pallas kernels for 0%

commit v1 on v0

--- a/solution.py
+++ b/solution.py
@@ -81,7 +81,12 @@
     middle = unit_rms(normed_f + mix_rates[0] * (unit_rms(attention) - normed_f)).astype(
         jnp.bfloat16
     )
-    sequence_mid = lax.all_gather(middle, "seq", axis=0, tiled=True)
+    ring = [middle]
+    for hop in range(3):
+        ring.append(lax.ppermute(ring[-1], "seq", [(dev, (dev + 1) % 4) for dev in range(4)]))
+    sequence_mid = jnp.roll(
+        jnp.concatenate(ring[::-1], axis=0), (lax.axis_index("seq") + 1) * ring[0].shape[0], axis=0
+    )
     columns = sequence_mid
     gate_up = jnp.einsum(
         "td,cdf->tcf",

time: 431 us -> 381 us (0.88)
  waiting for transfers between devices: 364 us -> 307 us
  local copies, waits for them, and re-layouts: 1.64 us -> 8.69 us
    all_gather x1, waiting for transfers between devices: 90.3 us -> 37.2 us  [on_device(): lax.all_gather(gate_up_weight, 'dp', axis=1, tiled=True)]
    all_gather x1 -> x0, waiting for transfers between devices: 43.4 us -> none  [on_device(): sequence_mid = lax.all_gather(middle, 'seq', axis=0, tiled=True)]
    ppermute x0 -> x3, waiting for transfers between devices: none -> 41.9 us  [on_device(): lax.ppermute(ring[-1], 'seq', [(dev, (dev + 1) % 4) for dev in range(4)])]
    unnamed x13 -> x16, local copies, waits for them, and re-layouts: 1.6 us -> 7.8 us
  transfers between devices with their start and end apart: 8 -> 10, of which waited for: 8 -> 10; matrix products, arithmetic and copies ran while one was open for 5% -> 9% of each run, Pallas kernels for 0% -> 0%
where the time goes in v1:
time: 381 us; the launch traced here: 380 us
  waiting for transfers between devices  307 us (81%)
  matrix products  37.1 us (10%)
  between operations  13.6 us (4%)
  other arithmetic  12.7 us (3%)
  local copies, waits for them, and re-layouts  8.69 us (2%)
    all_gather x1, waiting for transfers between devices, on_device(): sequence = lax.all_gather(normed, 'seq', axis=0, tiled=True)  45.6 us
    reduce_scatter x1, waiting for transfers between devices, on_device(): lax.psum_scatter(jnp.dot(part_rows, down_all, preferred_element_type=jnp....  43.8 us
    all_gather x1, waiting for transfers between devices, on_device(): down_all = lax.all_gather(down_weight, 'dp', axis=1, tiled=True)  42.7 us
    reduce_scatter x1, waiting for transfers between devices, on_device(): lax.psum_scatter(jnp.dot(part_rows, out_cols_all, preferred_element_type=...  42.5 us
    ppermute x3, waiting for transfers between devices, on_device(): lax.ppermute(ring[-1], 'seq', [(dev, (dev + 1) % 4) for dev in range(4)])  41.9 us
    all_gather x1, waiting for transfers between devices, on_device(): lax.all_gather(gate_up_weight, 'dp', axis=1, tiled=True)  37.2 us
    all_gather x1, waiting for transfers between devices, on_device(): lax.all_gather(qkv_weight, 'dp', axis=1, tiled=True)  33.4 us
    all_gather x1, waiting for transfers between devices, on_device(): out_cols_all = lax.all_gather(out_weight, 'dp', axis=1, tiled=True)  18.5 us
  transfers between devices with their start and end apart: 10, of which 10 were waited for; matrix products, arithmetic and copies ran while one was open for 9% of the time, Pallas kernels for 0%

profile of v1, /device:TPU:0, one launch (start us, length us, event | category | flops | bytes accessed | tf_op | source)
XLA Modules:
  0.0 380.4 jit_solution(10532019302147414249)
XLA Ops:
  6.5 1.2 fusion.18
  7.8 2.0 fusion.19
  9.9 1.9 copy.9
  12.7 45.6 %all-gather.6.cloned.1.call-done = bf16[512,2048]{1,0:T(8,128)(2,1)} async-done(((bf16[128,2048]{1,0:T(8,128)(2,1)}), bf16[512,2048]{1,0:T(8,128)(2,1)}) %all-gather.6.cloned.1.call-update) | async-done | bytes 2097168 | tf_op jit(solution)/shard_map/all_gather | solution.py:57
  58.3 33.4 %all-gather.8.cloned.1.call-done = bf16[3,2048,256]{1,2,0:T(8,128)(2,1)} async-done(((bf16[3,256,256]{1,2,0:T(8,128)(2,1)}), bf16[3,2048,256]{1,2,0:T(8,128)(2,1)}) %all-gather.8.cloned.1.call-update) | async-done | bytes 3145744 | tf_op jit(solution)/shard_map/all_gather | solution.py:63
  91.8 4.3 %fusion.7 = f32[512,3,256]{0,2,1:T(8,128)S(1)} fusion(bf16[3,2048,256]{1,2,0:T(8,128)(2,1)} %all-gather.8.cloned.1.call-done, bf16[512,2048]{1,0:T(8,128)(2,1)} %all-gather.6.cloned.1.call-done), kind=kOutput, calls=%fused_computation.11 | convolution fusion | flops 1610612736 | bytes 6815744 | tf_op jit(solution)/shard_map/td,cdn->tcn/dot_general | solution.py:60
  96.3 1.1 fusion.65
  97.3 1.4 convolution_convert_fusion.2
  98.7 18.5 %all-gather.10.cloned.1.call-done = bf16[256,2048]{1,0:T(8,128)(2,1)} async-done(((bf16[256,256]{1,0:T(8,128)(2,1)}), bf16[256,2048]{1,0:T(8,128)(2,1)}) %all-gather.10.cloned.1.call-update) | async-done | bytes 1048592 | tf_op jit(solution)/shard_map/all_gather | solution.py:72
  117.2 3.4 convolution_convert_fusion
  121.9 42.5 %reduce-scatter.3.cloned.1.call-done = bf16[128,2048]{1,0:T(8,128)(2,1)} async-done(((bf16[512,2048]{1,0:T(8,128)(2,1)}), bf16[128,2048]{1,0:T(8,128)(2,1)}) %reduce-scatter.3.cloned.1.call-update) | async-done | bytes 524304 | tf_op jit(solution)/shard_map/reduce_scatter | solution.py:74
  164.4 1.2 fusion.15
  165.7 1.5 multiply_reduce_fusion.1
  167.2 1.4 multiply_convert_fusion.1
  169.3 14.4 %collective-permute-done = bf16[128,2048]{1,0:T(8,128)(2,1)S(1)} collective-permute-done((bf16[128,2048]{1,0:T(8,128)(2,1)S(1)}, bf16[128,2048]{1,0:T(8,128)(2,1)S(1)}, u32[]{:S(2)}, u32[]{:S(2)}) %collective-permute-start) | collective-permute-done | bytes 524320 | tf_op jit(solution)/shard_map/ppermute | solution.py:86
  183.7 14.2 %collective-permute-done.1 = bf16[128,2048]{1,0:T(8,128)(2,1)S(1)} collective-permute-done((bf16[128,2048]{1,0:T(8,128)(2,1)S(1)}, bf16[128,2048]{1,0:T(8,128)(2,1)S(1)}, u32[]{:S(2)}, u32[]{:S(2)}) %collective-permute-start.1) | collective-permute-done | bytes 524320 | tf_op jit(solution)/shard_map/ppermute | solution.py:86
  198.0 13.3 %collective-permute-done.2 = bf16[128,2048]{1,0:T(8,128)(2,1)S(1)} collective-permute-done((bf16[128,2048]{1,0:T(8,128)(2,1)S(1)}, bf16[128,2048]{1,0:T(8,128)(2,1)S(1)}, u32[]{:S(2)}, u32[]{:S(2)}) %collective-permute-start.2) | collective-permute-done | bytes 524320 | tf_op jit(solution)/shard_map/ppermute | solution.py:86
  211.3 0.8 constant_dynamic-update-slice_fusion.7
  212.1 0.8 constant_dynamic-update-slice_fusion.6
  213.0 0.8 constant_dynamic-update-slice_fusion.5
  213.8 0.8 constant_dynamic-update-slice_fusion.4
  214.6 0.8 constant_dynamic-update-slice_fusion.3
  215.5 0.8 constant_dynamic-update-slice_fusion.2
  217.1 0.8 constant_dynamic-update-slice_fusion
  218.0 37.2 %all-gather.12.cloned.1.call-done = bf16[2,2048,2048]{2,1,0:T(8,128)(2,1)} async-done(((bf16[2,256,2048]{2,1,0:T(8,128)(2,1)}), bf16[2,2048,2048]{2,1,0:T(8,128)(2,1)}) %all-gather.12.cloned.1.call-update) | async-done | bytes 16777232 | tf_op jit(solution)/shard_map/all_gather | solution.py:94
  255.1 14.9 %fusion.5 = f32[512,2,2048]{2,0,1:T(8,128)} fusion(bf16[2,2048,2048]{2,1,0:T(8,128)(2,1)} %all-gather.12.cloned.1.call-done, bf16[1024,2048]{1,0:T(8,128)(2,1)} %constant_dynamic-update-slice_fusion, s32[]{:T(128)S(6)} %select_n.24), kind=kOutput, calls=%fused_computation.9 | convolution fusion | flops 8589934592 | bytes 27262980 | tf_op jit(solution)/shard_map/td,cdf->tcf/dot_general | solution.py:91
  270.1 42.7 %all-gather.14.cloned.1.call-done = bf16[2048,2048]{1,0:T(8,128)(2,1)} async-done(((bf16[2048,256]{1,0:T(8,128)(2,1)}), bf16[2048,2048]{1,0:T(8,128)(2,1)}) %all-gather.14.cloned.1.call-update) | async-done | bytes 8388624 | tf_op jit(solution)/shard_map/all_gather | solution.py:100
  312.8 11.9 %convolution_convert_fusion.1 = bf16[512,2048]{1,0:T(8,128)(2,1)} fusion(bf16[2048,2048]{1,0:T(8,128)(2,1)} %all-gather.14.cloned.1.call-done, f32[512,2,2048]{2,0,1:T(8,128)} %fusion.5, f32[2048]{0:T(1024)S(1)} %bitcast.89, f32[2048]{0:T(1024)S(1)} %bitcast.88), kind=kOutput, calls=%fused_computation.8 | convolution fusion | flops 4304404480 | bytes 18890752 | tf_op jit(solution)/shard_map/dot_general | solution.py:103
  324.7 43.8 %reduce-scatter.5.cloned.1.call-done = bf16[128,2048]{1,0:T(8,128)(2,1)} async-done(((bf16[512,2048]{1,0:T(8,128)(2,1)}), bf16[128,2048]{1,0:T(8,128)(2,1)}) %reduce-scatter.5.cloned.1.call-update) | async-done | bytes 524304 | tf_op jit(solution)/shard_map/reduce_scatter | solution.py:102
  368.5 1.2 fusion.17
  369.7 1.5 multiply_reduce_fusion
  371.2 2.3 fusion.23
  (37 shorter events, 3.9 us)
Async XLA Ops:
  6.5 6.1 %copy-start = (f32[1024]{0:T(1024)S(1)}, f32[1024]{0:T(1024)}, u32[]{:S(2)}) copy-start(f32[1024]{0:T(1024)} %param.10) | copy-start | bytes 12292
  6.5 51.8 %all-gather.6.cloned.1.call-start = ((), (), s32[]{:S(2)}) async-start(), calls=%async_computation.2 | async-start | bytes 2621440 | tf_op jit(solution)/shard_map/all_gather | solution.py:57
  9.8 82.0 %all-gather.8.cloned.1.call-start = ((), (), s32[]{:S(2)}) async-start(), calls=%async_computation.3 | async-start | bytes 3538944 | tf_op jit(solution)/shard_map/all_gather | solution.py:63
  11.8 105.3 %all-gather.10.cloned.1.call-start = ((), (), s32[]{:S(2)}) async-start(), calls=%async_computation.4 | async-start | bytes 1179648 | tf_op jit(solution)/shard_map/all_gather | solution.py:72
  12.6 151.9 %reduce-scatter.3.cloned.1.call-start = ((), (), s32[]{:S(2)}) async-start(), calls=%async_computation.5 | async-start | bytes 2621440 | tf_op jit(solution)/shard_map/reduce_scatter | solution.py:74
  117.2 4.7 %copy-start.2 = (f32[2,2048]{1,0:T(2,128)S(1)}, f32[2,2048]{1,0:T(2,128)}, u32[]{:S(2)}) copy-start(f32[2,2048]{1,0:T(2,128)} %param.12) | copy-start | bytes 49156
  117.2 48.5 %copy-start.1 = (bf16[1,128,2048]{2,1,0:T(8,128)(2,1)S(1)}, bf16[1,128,2048]{2,1,0:T(8,128)(2,1)}, u32[]{:S(2)}) copy-start(bf16[1,128,2048]{2,1,0:T(8,128)(2,1)} %param.8) | copy-start | bytes 1572868
  120.6 77.3 %copy-start.3 = (f32[2,2048]{1,0:T(2,128)S(1)}, f32[2,2048]{1,0:T(2,128)}, u32[]{:S(2)}) copy-start(f32[2,2048]{1,0:T(2,128)} %param.14) | copy-start | bytes 49156
  120.6 134.5 %all-gather.12.cloned.1.call-start = ((), (), s32[]{:S(2)}) async-start(), calls=%async_computation.6 | async-start | bytes 18874368 | tf_op jit(solution)/shard_map/all_gather | solution.py:94
  121.2 191.5 %all-gather.14.cloned.1.call-start = ((), (), s32[]{:S(2)}) async-start(), calls=%async_computation.7 | async-start | bytes 9437184 | tf_op jit(solution)/shard_map/all_gather | solution.py:100
  121.8 246.7 %reduce-scatter.5.cloned.1.call-start = ((), (), s32[]{:S(2)}) async-start(), calls=%async_computation.8 | async-start | bytes 2621440 | tf_op jit(solution)/shard_map/reduce_scatter | solution.py:102
  168.6 15.1 %collective-permute-start = (bf16[128,2048]{1,0:T(8,128)(2,1)S(1)}, bf16[128,2048]{1,0:T(8,128)(2,1)S(1)}, u32[]{:S(2)}, u32[]{:S(2)}) collective-permute-start(bf16[128,2048]{1,0:T(8,128)(2,1)S(1)} %multiply_convert_fusion.1), channel_id=1, source_target_pairs={{0,1},{1,2},{2,3},{3,0},{4,5},{5,6},{6,7},{7,4},{8,9},{9,10},{10,1... | collective-permute-start | bytes 1572872 | tf_op jit(solution)/shard_map/ppermute | solution.py:86
  183.7 14.2 %collective-permute-start.1 = (bf16[128,2048]{1,0:T(8,128)(2,1)S(1)}, bf16[128,2048]{1,0:T(8,128)(2,1)S(1)}, u32[]{:S(2)}, u32[]{:S(2)}) collective-permute-start(bf16[128,2048]{1,0:T(8,128)(2,1)S(1)} %collective-permute-done), channel_id=1, source_target_pairs={{0,1},{1,2},{2,3},{3,0},{4,5},{5,6},{6,7},{7,4},{8,9},{9,10},{10,1... | collective-permute-start | bytes 1572872 | tf_op jit(solution)/shard_map/ppermute | solution.py:86
  197.9 13.4 %collective-permute-start.2 = (bf16[128,2048]{1,0:T(8,128)(2,1)S(1)}, bf16[128,2048]{1,0:T(8,128)(2,1)S(1)}, u32[]{:S(2)}, u32[]{:S(2)}) collective-permute-start(bf16[128,2048]{1,0:T(8,128)(2,1)S(1)} %collective-permute-done.1), channel_id=1, source_target_pairs={{0,1},{1,2},{2,3},{3,0},{4,5},{5,6},{6,7},{7,4},{8,9},{9,10},{10,1... | collective-permute-start | bytes 1572872 | tf_op jit(solution)/shard_map/ppermute | solution.py:86
Sparse Core Ops, SparseCore 0:
  9.9 48.3 all-gather.5
  60.2 31.5 all-gather.7
  93.7 23.4 all-gather.9
  120.8 43.6 reduce-scatter.2
  166.2 88.9 all-gather.11
  256.9 55.8 all-gather.13
  324.9 43.5 reduce-scatter.4
